TPU v7x, 32 devices: a whole 2x2x4 slice. The times are simulated.
32 devices in a mesh: row: 4 (over z), col: 8 (over y, x, core).
Axes of the slice: x: 2, y: 2, z: 4, core: 2. Of those that a mesh axis runs over, the one named last changes fastest.
Arguments:
- latent: float32 [2, 1024, 2048], P(None, 'row', 'col'), may hold values from -3 to 3
- momentum: float32 [2, 1024, 2048], P(None, 'row', 'col'), may hold values from -4 to 4
- hyper_params: float32 [2, 2], replicated, may hold values from 0.3 to 0.7
- velocity: float32 [2, 2], replicated, may hold values from -3 to 3
- step_size: float32 [2], replicated, may hold values from 0.08 to 0.12
- counts: int32 [1024, 2048], P('row', 'col'), may hold values from 0 to 7
- kappa_field: float32 [1024, 2048], P('row', 'col'), may hold values from 0.1 to 1
Outputs:
- latent_out: float32 [2, 1024, 2048], P(None, 'row', 'col')
- momentum_out: float32 [2, 1024, 2048], P(None, 'row', 'col')
- hyper_out: float32 [2, 2], replicated
- velocity_out: float32 [2, 2], replicated
All inputs are finite; a program needn't handle non-finite values.
Results may differ from a plain program's by a relative error of at most 0.0001.
Values sent between devices are 32-bit elements; how exact they have to be, the bound alone decides.
A program may use at most 64 MiB of HBM per device.

v0:
```python
import functools

import jax
import jax.numpy as jnp
from jax import lax
from jax.experimental import pallas as pl
from jax.experimental.pallas import tpu as pltpu
from jax.sharding import PartitionSpec as P

STEPS = 10
HALO = 16
PAD = 8
TOP = PAD + HALO
LANES = 128
OWN_DEEP, SIDE_DEEP, KICK_DEEP, PACK_DEEP, UNPACK_DEEP = 256, 256, 48, 64, 96
SEG = 16
MESH = pl.DeviceIdType.MESH


def kernel(
    sizes, latent, momentum, counts, kappa, hyper, velocity, step_size,
    latent_out, momentum_out, hyper_out, velocity_out,
    state, diagonal, applied, intensity, raw_counts, left_pack, right_pack, from_right, from_left,
    payload, gathered,
    load_sem, store_sem, halo_send, halo_recv, sum_send, sum_recv,
):
    nr, nc, chains, rows, tiles, total = sizes
    devices = nr * nc
    row, col = lax.axis_index("row"), lax.axis_index("col")
    me = row * nc + col
    arrays = 2 * chains + 2
    kap, cnt = 2 * chains, 2 * chains + 1
    own = pl.ds(TOP, rows)

    loads = []
    for c in range(chains):
        for j in range(tiles):
            cols = pl.ds(j * LANES, LANES)
            loads.append((latent.at[c, :, cols], state.at[c, j, own, :]))
            loads.append((momentum.at[c, :, cols], state.at[chains + c, j, own, :]))
    for j in range(tiles):
        cols = pl.ds(j * LANES, LANES)
        loads.append((kappa.at[:, cols], state.at[kap, j, own, :]))
        loads.append((counts.at[:, cols], raw_counts.at[j]))
    loads = [pltpu.make_async_copy(s, d, load_sem.at[i]) for i, (s, d) in enumerate(loads)]
    for copy in loads:
        copy.start()

    def peer(d):
        other = lax.rem(me + d, devices)
        return (other // nc, lax.rem(other, nc))

    barrier = pltpu.get_barrier_semaphore()
    for d in sorted(range(1, devices), key=lambda d: -min(d, devices - d)):
        pl.semaphore_signal(barrier, inc=1, device_id=peer(d), device_id_type=MESH)

    lane = lax.broadcasted_iota(jnp.int32, (8, LANES), 1)
    seg = lane // SEG
    sublane = lax.broadcasted_iota(jnp.int32, (8, LANES), 0)
    first = lax.broadcasted_iota(jnp.int32, (1, LANES), 1) == 0
    last = lax.broadcasted_iota(jnp.int32, (1, LANES), 1) == LANES - 1

    for copy in loads:
        copy.wait()

    def pack(i, counted):
        rel = pl.ds(pl.multiple_of(i * PACK_DEEP, 8), PACK_DEEP)
        here = pl.ds(pl.multiple_of(TOP + i * PACK_DEEP, 8), PACK_DEEP)
        value = [raw_counts[j, rel, :].astype(jnp.float32) for j in range(tiles)]
        heads = [state[a, 0, here, :] for a in range(arrays - 1)] + [value[0]]
        tails = [state[a, tiles - 1, here, :] for a in range(arrays - 1)] + [value[-1]]
        lp, rp = heads[0], pltpu.roll(tails[0], SEG, 1)
        for a in range(1, arrays):
            lp = jnp.where(seg[:1] == a, pltpu.roll(heads[a], SEG * a, 1), lp)
            rp = jnp.where(seg[:1] == a, pltpu.roll(tails[a], SEG * (a + 1) % LANES, 1), rp)
        left_pack[rel, :] = lp
        right_pack[rel, :] = rp
        for j in range(tiles):
            state[cnt, j, here, :] = value[j]
        both = sum(value)
        return counted + sum(both[8 * u : 8 * u + 8] for u in range(PACK_DEEP // 8))

    zeros = jnp.zeros((8, LANES), jnp.float32)
    counted = lax.fori_loop(0, rows // PACK_DEEP, pack, zeros)

    pl.semaphore_wait(barrier, devices - 1)

    up, down = lax.rem(row + nr - 1, nr), lax.rem(row + 1, nr)
    left, right = lax.rem(col + nc - 1, nc), lax.rem(col + 1, nc)
    head, tail = pl.ds(0, HALO), pl.ds(rows - HALO, HALO)
    body, below = pl.ds(HALO, rows), pl.ds(HALO + rows, HALO)
    halos = [
        (left_pack.at[:, :], from_right.at[body, :], (row, left)),
        (right_pack.at[:, :], from_left.at[body, :], (row, right)),
        (
            state.at[:, pl.ds(0, tiles), pl.ds(TOP, HALO), :],
            state.at[:, pl.ds(0, tiles), pl.ds(TOP + rows, HALO), :],
            (up, col),
        ),
        (
            state.at[:, pl.ds(0, tiles), pl.ds(TOP + rows - HALO, HALO), :],
            state.at[:, pl.ds(0, tiles), pl.ds(PAD, HALO), :],
            (down, col),
        ),
        (left_pack.at[tail, :], from_right.at[head, :], (down, left)),
        (left_pack.at[head, :], from_right.at[below, :], (up, left)),
        (right_pack.at[tail, :], from_left.at[head, :], (down, right)),
        (right_pack.at[head, :], from_left.at[below, :], (up, right)),
    ]
    halos = [
        pltpu.make_async_remote_copy(
            src_ref=s, dst_ref=d, send_sem=halo_send.at[i], recv_sem=halo_recv.at[i],
            device_id=where, device_id_type=MESH,
        )
        for i, (s, d, where) in enumerate(halos)
    ]
    for copy in halos:
        copy.start()
    for copy in halos:
        copy.wait()

    def unpack(i, carry):
        rel = pl.ds(pl.multiple_of(i * UNPACK_DEEP, 8), UNPACK_DEEP)
        here = pl.ds(pl.multiple_of(PAD + i * UNPACK_DEEP, 8), UNPACK_DEEP)
        fr, fl = from_right[rel, :], from_left[rel, :]
        values = []
        for a in range(arrays):
            right_part = pltpu.roll(fr, (LANES - SEG * a) % LANES, 1) if a else fr
            left_part = pltpu.roll(fl, (LANES - SEG * (a + 1)) % LANES, 1)
            left_part = jnp.where(seg[:1] == 7, left_part, 0.0)
            values.append(jnp.where(seg[:1] == 0, right_part, left_part))
        plus = [state[kap, j, here, :] + 4.0 for j in range(tiles)] + [values[kap] + 4.0]
        for a in range(arrays):
            state[a, tiles, here, :] = values[a]
        for j in range(tiles + 1):
            diagonal[j, here, :] = plus[j]
        return carry

    lax.fori_loop(0, (rows + 2 * HALO) // UNPACK_DEEP, unpack, 0)

    def stencil_tiles(r, deep, lane_tiles):
        rowset = pl.ds(r, deep)
        terms, results = [], []
        for c in range(chains):
            full = [state[c, j, rowset, :] for j in range(tiles + 1)]
            used = sorted({(j + s) % (tiles + 1) for j in lane_tiles for s in (-1, 0)})
            to_right = {j: pltpu.roll(full[j], 1, 1) for j in used}
            used = sorted({(j + s) % (tiles + 1) for j in lane_tiles for s in (1, 0)})
            to_left = {j: pltpu.roll(full[j], LANES - 1, 1) for j in used}
            quad = mass = None
            for j in lane_tiles:
                v = full[j]
                beside = jnp.where(first, to_right[(j - 1) % (tiles + 1)], to_right[j])
                beside += jnp.where(last, to_left[(j + 1) % (tiles + 1)], to_left[j])
                beside += state[c, j, pl.ds(r - 1, deep), :] + state[c, j, pl.ds(r + 1, deep), :]
                av = diagonal[j, rowset, :] * v - beside
                ex = jnp.exp(v)
                results.append((c, j, av, ex))
                quad = v * av if quad is None else quad + v * av
                mass = ex if mass is None else mass + ex
            terms += [quad, mass]
        for c, j, av, ex in results:
            applied[c, j, rowset, :] = av
            intensity[c, j, rowset, :] = ex
        return [sum(t[8 * u : 8 * u + 8] for u in range(deep // 8)) for t in terms]

    def own_part():
        def body(i, sums):
            r = pl.multiple_of(TOP + i * OWN_DEEP, 8)
            terms = stencil_tiles(r, OWN_DEEP, range(tiles))
            return tuple(s + t for s, t in zip(sums, terms))

        zero = jnp.zeros((8, LANES), jnp.float32)
        return lax.fori_loop(0, rows // OWN_DEEP, body, (zero,) * (2 * chains))

    def halo_part():
        def side(i, carry):
            stencil_tiles(pl.multiple_of(TOP + i * SIDE_DEEP, 8), SIDE_DEEP, [tiles])
            return carry

        lax.fori_loop(0, rows // SIDE_DEEP, side, 0)
        stencil_tiles(PAD, HALO, range(tiles + 1))
        stencil_tiles(TOP + rows, HALO, range(tiles + 1))

    def whole(x):
        return jnp.sum(jnp.sum(x, axis=0, keepdims=True), axis=1, keepdims=True)

    counted = whole(counted)

    def send(k, sums):
        q0, e0, q1, e1 = [whole(s) for s in sums]
        out = counted
        for i, value in enumerate((q0, q1, e0, e1)):
            out = jnp.where(seg[:1] == i, value, out)
        payload[k] = out
        gathered[k, me] = out
        for d in sorted(range(1, devices), key=lambda d: -min(d, devices - d)):
            pltpu.make_async_remote_copy(
                src_ref=payload.at[k], dst_ref=gathered.at[k, me],
                send_sem=sum_send.at[k], recv_sem=sum_recv.at[k],
                device_id=peer(d), device_id_type=MESH,
            ).start()

    def collect(k):
        bulk = gathered.at[k, pl.ds(0, devices - 1)]
        copy = pltpu.make_async_remote_copy(
            src_ref=bulk, dst_ref=bulk, send_sem=sum_send.at[k], recv_sem=sum_recv.at[k],
            device_id=peer(1), device_id_type=MESH,
        )
        copy.wait_recv()
        return jnp.broadcast_to(jnp.sum(gathered[k], axis=0), (8, LANES))

    def spread(values):
        out = jnp.zeros((8, LANES), jnp.float32)
        for i, value in enumerate(values):
            out = jnp.where(seg == i, value, out)
        return out

    h = [step_size[c] for c in range(chains)]
    hvec = spread([h[0], h[1], h[0], h[1]])
    hyp = spread([hyper[1, 0], hyper[1, 1], hyper[0, 0], hyper[0, 1]])
    vel = spread([velocity[1, 0], velocity[1, 1], velocity[0, 0], velocity[0, 1]])
    is_quad = seg < 2
    coef = jnp.where(is_quad, 0.5 / total, 1.0 / total)

    def accel(summed, expd):
        target = pltpu.roll(summed, LANES - 2 * SEG, 1) * (1.0 / total)
        return coef * expd * summed - jnp.where(is_quad, 0.5, target)

    def pick(x, i):
        return jnp.sum(jnp.where(lane == i * SEG, x, 0.0), axis=1, keepdims=True)

    def weights(expd, scale):
        scaled = expd * hvec * scale
        return [jnp.broadcast_to(pick(scaled, i)[:1], (1, LANES)) for i in range(2 * chains)]

    def kick(r, deep, c, j, w, scale):
        rowset = pl.ds(r, deep)
        m = state[chains + c, j, rowset, :] + (h[c] * scale) * state[cnt, j, rowset, :]
        return m - w[c] * applied[c, j, rowset, :] - w[chains + c] * intensity[c, j, rowset, :]

    def advance(w, scale):
        def body(i, carry):
            rowset = pl.ds(pl.multiple_of(PAD + i * KICK_DEEP, 8), KICK_DEEP)
            moved = []
            for c in range(chains):
                for j in range(tiles + 1):
                    m = kick(rowset.start, KICK_DEEP, c, j, w, scale)
                    moved.append((c, j, m, state[c, j, rowset, :] + h[c] * m))
            for c, j, m, v in moved:
                state[chains + c, j, rowset, :] = m
                state[c, j, rowset, :] = v
            return carry

        lax.fori_loop(0, (rows + 2 * HALO) // KICK_DEEP, body, 0)

    def round_of(k):
        sums = own_part()
        send(k, sums)

    expd = jnp.exp(hyp)
    round_of(0)
    halo_part()
    advance(weights(expd, 0.5), 0.5)
    round_of(1)

    def step(k, carry):
        hyp, vel, expd = carry
        halo_part()
        a = accel(collect(k - 1), expd)
        vel = vel - jnp.where(k == 1, 0.5, 1.0) * hvec * a
        hyp = hyp + hvec * vel
        expd = jnp.exp(hyp)
        advance(weights(expd, 1.0), 1.0)
        round_of(k + 1)
        return hyp, vel, expd

    hyp, vel, expd = lax.fori_loop(1, STEPS, step, (hyp, vel, expd))

    def stores(base, out, start):
        copies = []
        for c in range(chains):
            for j in range(tiles):
                cols = pl.ds(j * LANES, LANES)
                copies.append(
                    pltpu.make_async_copy(
                        state.at[base + c, j, own, :],
                        out.at[c, :, cols],
                        store_sem.at[start + len(copies)],
                    )
                )
        for copy in copies:
            copy.start()
        return copies

    pending = stores(0, latent_out, 0)
    vel = vel - hvec * accel(collect(STEPS - 1), expd)
    hyp = hyp + hvec * vel
    expd = jnp.exp(hyp)
    w = weights(expd, 0.5)

    def final(i, carry):
        rowset = pl.ds(pl.multiple_of(TOP + i * PACK_DEEP, 8), PACK_DEEP)
        moved = []
        for c in range(chains):
            for j in range(tiles):
                moved.append((c, j, kick(rowset.start, PACK_DEEP, c, j, w, 0.5)))
        for c, j, m in moved:
            state[chains + c, j, rowset, :] = m
        return carry

    lax.fori_loop(0, rows // PACK_DEEP, final, 0)
    pending += stores(chains, momentum_out, len(pending))
    vel = vel - 0.5 * hvec * accel(collect(STEPS), expd)

    out_row, out_col = sublane[:2, :2], lane[:2, :2]
    for x, ref in ((hyp, hyper_out), (vel, velocity_out)):
        picks = [pick(x, i)[:2] for i in range(2 * chains)]
        low = jnp.where(out_col == 0, picks[2], picks[3])
        high = jnp.where(out_col == 0, picks[0], picks[1])
        ref[...] = jnp.where(out_row == 0, low, high)
    for copy in pending:
        copy.wait()

    def drain(k, carry):
        bulk = gathered.at[k, pl.ds(0, devices - 1)]
        pltpu.make_async_remote_copy(
            src_ref=bulk, dst_ref=bulk, send_sem=sum_send.at[k], recv_sem=sum_recv.at[k],
            device_id=peer(1), device_id_type=MESH,
        ).wait_send()
        return carry

    lax.fori_loop(0, STEPS + 1, drain, 0)


def hand_out(latent, momentum, hyper, velocity, latent_out, momentum_out, hyper_out, velocity_out, sems):
    copies = [
        pltpu.make_async_copy(latent, latent_out, sems.at[0]),
        pltpu.make_async_copy(momentum, momentum_out, sems.at[1]),
    ]
    for copy in copies:
        copy.start()
    hyper_out[...] = hyper[...]
    velocity_out[...] = velocity[...]
    for copy in copies:
        copy.wait()


def solution(mesh):
    nr, nc = mesh.shape["row"], mesh.shape["col"]
    devices = nr * nc

    def shards(latent, momentum, hyper_params, velocity, step_size, counts, kappa_field):
        chains, rows, cols = latent.shape
        tiles = cols // LANES
        deep = rows + 2 * TOP
        total = float(rows * nr * cols * nc)
        sizes = (nr, nc, chains, rows, tiles, total)
        anywhere = pl.BlockSpec(memory_space=pl.ANY)
        scalars = pl.BlockSpec(memory_space=pltpu.SMEM)
        small = pl.BlockSpec(memory_space=pltpu.VMEM)
        arrays = 2 * chains + 2
        f32 = jnp.float32
        results = pl.pallas_call(
            functools.partial(kernel, sizes),
            out_shape=(
                jax.ShapeDtypeStruct(latent.shape, f32),
                jax.ShapeDtypeStruct(latent.shape, f32),
                jax.ShapeDtypeStruct(hyper_params.shape, f32),
                jax.ShapeDtypeStruct(velocity.shape, f32),
            ),
            in_specs=[anywhere] * 4 + [scalars] * 3,
            out_specs=(anywhere, anywhere, small, small),
            scratch_shapes=[
                pltpu.VMEM((arrays, tiles + 1, deep, LANES), f32),
                pltpu.VMEM((tiles + 1, deep, LANES), f32),
                pltpu.VMEM((chains, tiles + 1, deep, LANES), f32),
                pltpu.VMEM((chains, tiles + 1, deep, LANES), f32),
                pltpu.VMEM((tiles, rows, LANES), jnp.int32),
                pltpu.VMEM((rows, LANES), f32),
                pltpu.VMEM((rows, LANES), f32),
                pltpu.VMEM((rows + 2 * HALO, LANES), f32),
                pltpu.VMEM((rows + 2 * HALO, LANES), f32),
                pltpu.VMEM((STEPS + 1, 1, LANES), f32),
                pltpu.VMEM((STEPS + 1, devices, 1, LANES), f32),
                pltpu.SemaphoreType.DMA((2 * tiles * (chains + 1),)),
                pltpu.SemaphoreType.DMA((2 * tiles * chains,)),
                pltpu.SemaphoreType.DMA((8,)),
                pltpu.SemaphoreType.DMA((8,)),
                pltpu.SemaphoreType.DMA((STEPS + 1,)),
                pltpu.SemaphoreType.DMA((STEPS + 1,)),
            ],
            compiler_params=pltpu.CompilerParams(collective_id=0, has_side_effects=True),
        )(latent, momentum, counts, kappa_field, hyper_params, velocity, step_size)
        return pl.pallas_call(
            hand_out,
            out_shape=[jax.ShapeDtypeStruct(x.shape, f32) for x in results],
            in_specs=[small] * 4,
            out_specs=[anywhere] * 2 + [small] * 2,
            scratch_shapes=[pltpu.SemaphoreType.DMA((2,))],
        )(*results)

    placed = (
        P(None, "row", "col"),
        P(None, "row", "col"),
        P(),
        P(),
        P(),
        P("row", "col"),
        P("row", "col"),
    )
    return jax.shard_map(
        shards,
        mesh=mesh,
        in_specs=placed,
        out_specs=(P(None, "row", "col"), P(None, "row", "col"), P(), P()),
        check_vma=False,
    )
```

profile of v0, /device:TPU:0, one launch (start us, length us, event | category | flops | bytes accessed | tf_op | source)
XLA Modules:
  0.0 53.0 jit_solution(4283854074637501799)
XLA Ops:
  0.6 49.7 %shard_map.102 = (f32[2,256,256]{2,1,0:T(8,128)}, f32[2,256,256]{2,1,0:T(8,128)}, f32[2,2]{1,0:T(2,128)}, f32[2,2]{1,0:T(2,128)}) custom-call(f32[2,256,256]{2,1,0:T(8,128)} %latent.1, f32[2,256,256]{2,1,0:T(8,128)} %momentum.1, s32[256,256]{1,0:T(8,128)} %counts.1, f32[256,256]{1,0:T(8,128)} %kappa.1, f32[2,2]{1,0:T(2,128)} %hyper.1, f32[2,2]{1,0:T(2,128)} %velocity.1, ...), custom_call_target="tpu_custom_call" | custom-call | tf_op jit(solution)/shard_map/pallas_call | solution.py:364
  50.3 2.8 %shard_map.103 = (f32[2,256,256]{2,1,0:T(8,128)}, f32[2,256,256]{2,1,0:T(8,128)}, f32[2,2]{1,0:T(2,128)}, f32[2,2]{1,0:T(2,128)}) custom-call(f32[2,256,256]{2,1,0:T(8,128)} %get-tuple-element.8.latent, f32[2,256,256]{2,1,0:T(8,128)} %get-tuple-element.9.momentum, f32[2,2]{1,0:T(2,128)} %get-tuple-element.10.hyper, f32[2,2]{1,0:T(2,128)} %get-tuple-element.11.velocity), custom_call_target="tpu_custom_call" | custom-call | tf_op jit(solution)/shard_map/pallas_call | solution.py:395
where the time goes:
time: 53.2 us; the launch traced here: 53 us
  Pallas kernels  52.4 us (98%)
  between operations  0.64 us (1%)
    pallas_call x1, Pallas kernels, shards(): pl.pallas_call(functools.partial(kernel, sizes), out_shape=(jax.ShapeDtyp...  49.7 us
    pallas_call x1, Pallas kernels, shards(): pl.pallas_call(hand_out, out_shape=[jax.ShapeDtypeStruct(x.shape, f32) fo...  2.75 us

commit v1 on v0

v1 whole, which is shorter than its diff:
```python
import functools

import jax
import jax.numpy as jnp
from jax import lax
from jax.experimental import pallas as pl
from jax.experimental.pallas import tpu as pltpu
from jax.sharding import PartitionSpec as P

STEPS = 10
HALO = 16
EDGE = 8
PAD = 8
TOP = PAD + HALO
LANES = 128
SEG = 16
MESH = pl.DeviceIdType.MESH
COEFS = 6


def signal_rounds(nr, nc):
    rounds, reach = [], 1
    while reach < nr // 2 or reach < nc // 2:
        rs = (0, reach, -reach) if reach < nr // 2 else (0,)
        cs = (0, reach, -reach) if reach < nc // 2 else (0,)
        rounds.append([(r, c) for r in rs for c in cs if (r, c) != (0, 0)])
        reach *= 2
    return rounds


def kernel(
    sizes, latent, momentum, counts, kappa, hyper_in, velocity_in, step_in,
    latent_out, momentum_out, hyper_out, velocity_out,
    state, field_u, diagonal, applied, intensity, scaled, scaled_applied, fresh, raw_counts,
    pack_one, pack_two, take_one, take_two, corner_one, corner_two,
    payload, gathered, scal, hyper, velocity, step_size,
    load_sem, halo_send, halo_recv, sum_send, sum_recv, round_sem,
):
    nr, nc, chains, rows, tiles, total = sizes
    devices = nr * nc
    row, col = lax.axis_index("row"), lax.axis_index("col")
    me = row * nc + col
    kap, cnt = 2 * chains, 2 * chains + 1
    fold_one, fold_two = LANES // (SEG * chains), LANES // (SEG * (chains + 2))
    rows_one, rows_two = rows // fold_one, rows // fold_two
    own = pl.ds(TOP, rows)
    everything = range(tiles + 1)

    smalls = [(hyper_in, hyper), (velocity_in, velocity), (step_in, step_size)]
    vloads, loads = [], []
    for c in range(chains):
        for j in range(tiles):
            cols = pl.ds(j * LANES, LANES)
            vloads.append((latent.at[c, :, cols], state.at[c, j, own, :]))
            loads.append((momentum.at[c, :, cols], state.at[chains + c, j, own, :]))
    for j in range(tiles):
        cols = pl.ds(j * LANES, LANES)
        loads.append((kappa.at[:, cols], state.at[kap, j, own, :]))
        loads.append((counts.at[:, cols], raw_counts.at[j]))
    first_loads = len(vloads)
    loads = [
        pltpu.make_async_copy(s, d, load_sem.at[i]) for i, (s, d) in enumerate(vloads + loads + smalls)
    ]
    for copy in loads:
        copy.start()

    def at(dr, dc):
        return (lax.rem(row + (dr + nr), nr), lax.rem(col + (dc + nc), nc))

    near = [(r, c) for r in (0, 1, -1) for c in (0, 1, -1) if (r, c) != (0, 0)]
    barrier = pltpu.get_barrier_semaphore()
    for r, c in near:
        pl.semaphore_signal(barrier, inc=1, device_id=at(r, c), device_id_type=MESH)

    lane = lax.broadcasted_iota(jnp.int32, (8, LANES), 1)
    sublane = lax.broadcasted_iota(jnp.int32, (8, LANES), 0)
    lane_row = lax.broadcasted_iota(jnp.int32, (1, LANES), 1)
    seg = lane_row // SEG
    first, last = lane_row == 0, lane_row == LANES - 1

    def fold(x):
        return sum(x[8 * i : 8 * i + 8] for i in range(x.shape[0] // 8))

    def whole(x):
        return jnp.broadcast_to(jnp.sum(jnp.sum(x, axis=0, keepdims=True), axis=1, keepdims=True), (8, LANES))

    def pack(ref, arrays, depth, folds):
        heads = tails = None
        for s in range(folds):
            part = pl.ds(TOP + s * depth, depth)
            for i, a in enumerate(arrays):
                slot = s * len(arrays) + i
                head, tail = state[a, 0, part, :], state[a, tiles - 1, part, :]
                if slot:
                    head = pltpu.roll(head, slot * SEG, 1)
                tail = pltpu.roll(tail, (slot + 1) * SEG % LANES, 1) if (slot + 1) * SEG % LANES else tail
                heads = head if heads is None else jnp.where(seg == slot, head, heads)
                tails = tail if tails is None else jnp.where(seg == slot, tail, tails)
        ref[0] = heads
        ref[1] = tails

    def unpack(right, left, slot_right, slot_left):
        turn = (LANES - SEG * slot_right) % LANES
        right = pltpu.roll(right, turn, 1) if turn else right
        turn = (LANES - SEG - SEG * slot_left) % LANES
        left = pltpu.roll(left, turn, 1) if turn else left
        return jnp.where(seg == 0, right, jnp.where(seg == LANES // SEG - 1, left, 0.0))

    for copy in loads[:first_loads]:
        copy.wait()
    pack(pack_one, list(range(chains)), rows_one, fold_one)
    pl.semaphore_wait(barrier, len(near))

    remotes = []

    def remote(src, dst, where):
        copy = pltpu.make_async_remote_copy(
            src_ref=src, dst_ref=dst, send_sem=halo_send.at[len(remotes)], recv_sem=halo_recv.at[len(remotes)],
            device_id=where, device_id_type=MESH,
        )
        remotes.append(copy)
        copy.start()

    vs, rest = pl.ds(0, chains), pl.ds(chains, chains + 2)
    flat = pl.ds(0, tiles)

    def rowcopies(arrays, near_row, depth):
        remote(
            state.at[arrays, flat, pl.ds(TOP + near_row, depth), :],
            state.at[arrays, flat, pl.ds(TOP + rows + near_row, depth), :],
            at(-1, 0),
        )
        remote(
            state.at[arrays, flat, pl.ds(TOP + rows - near_row - depth, depth), :],
            state.at[arrays, flat, pl.ds(TOP - near_row - depth, depth), :],
            at(1, 0),
        )

    remote(pack_one.at[0], take_one.at[0], at(0, -1))
    remote(pack_one.at[1], take_one.at[1], at(0, 1))
    rowcopies(vs, 0, EDGE)
    stage_one = len(remotes)

    rounds = signal_rounds(nr, nc)

    def tell(i):
        for r, c in rounds[i]:
            pl.semaphore_signal(round_sem.at[i], inc=1, device_id=at(r, c), device_id_type=MESH)

    tell(0)

    for copy in loads[first_loads:]:
        copy.wait()
    counted = jnp.zeros((8, LANES), jnp.float32)
    for j in range(tiles):
        value = raw_counts[j].astype(jnp.float32)
        state[cnt, j, own, :] = value
        counted += fold(value)
    pack(pack_two, list(range(chains, 2 * chains + 2)), rows_two, fold_two)
    rowcopies(vs, EDGE, HALO - EDGE)
    remote(pack_two.at[0], take_two.at[0], at(0, -1))
    remote(pack_two.at[1], take_two.at[1], at(0, 1))
    rowcopies(rest, 0, HALO)
    for side, dc in ((0, -1), (1, 1)):
        for vert, dr in ((1, -1), (0, 1)):
            for mine, theirs, deep in ((pack_one, corner_one, rows_one), (pack_two, corner_two, rows_two)):
                start = 0 if vert else deep - HALO
                remote(mine.at[side, pl.ds(start, HALO)], theirs.at[side, vert], at(dr, dc))

    h = [step_size[c] for c in range(chains)]
    hh = [h[c] * h[c] for c in range(chains)]

    def full(value):
        return jnp.full((8, LANES), value, jnp.float32)

    TAU, EXO, HYQ, HYE, VEQ, VEE = (i * chains for i in range(6))
    CO = 6 * chains
    LOCAL = CO + COEFS * chains
    for c in range(chains):
        scal[HYQ + c] = full(hyper[1, c])
        scal[HYE + c] = full(hyper[0, c])
        scal[VEQ + c] = full(velocity[1, c])
        scal[VEE + c] = full(velocity[0, c])
        scal[TAU + c] = jnp.exp(full(hyper[1, c]))
        scal[EXO + c] = jnp.exp(full(hyper[0, c]))
    scal[LOCAL] = whole(counted)

    mass = []
    for c in range(chains):
        acc = None
        for j in range(tiles):
            value = jnp.exp(state[c, j, own, :])
            intensity[c, j, own, :] = value
            acc = fold(value) if acc is None else acc + fold(value)
        mass.append(whole(acc))
    for j in range(tiles):
        diagonal[j, own, :] = state[kap, j, own, :] + 4.0
        for c in range(chains):
            hc = hh[c] * state[cnt, j, own, :]
            scaled[c, j, own, :] = hc
            field_u[c, j, own, :] = state[c, j, own, :] + (h[c] * state[chains + c, j, own, :] + 0.5 * hc)

    def stencil(ref, c, r, deep, lane_tiles):
        rowset = pl.ds(r, deep)
        at_tile = [ref[c, j, rowset, :] for j in everything]
        n = tiles + 1
        used = sorted({(j + s) % n for j in lane_tiles for s in (-1, 0)})
        to_right = {j: pltpu.roll(at_tile[j], 1, 1) for j in used}
        used = sorted({(j + s) % n for j in lane_tiles for s in (1, 0)})
        to_left = {j: pltpu.roll(at_tile[j], LANES - 1, 1) for j in used}
        out = []
        for j in lane_tiles:
            beside = jnp.where(first, to_right[(j - 1) % n], to_right[j])
            beside += jnp.where(last, to_left[(j + 1) % n], to_left[j])
            beside += ref[c, j, pl.ds(r - 1, deep), :] + ref[c, j, pl.ds(r + 1, deep), :]
            out.append((j, at_tile[j], diagonal[j, rowset, :] * at_tile[j] - beside))
        return out

    DEEP = 64

    def own_blocks():
        return [TOP + i * DEEP for i in range(rows // DEEP)]

    def sides():
        out = [(TOP + i * DEEP, DEEP, [tiles]) for i in range(rows // DEEP)]
        return out + [(PAD, HALO, everything), (TOP + rows, HALO, everything)]

    def own_applied():
        quads = []
        for c in range(chains):
            acc = jnp.zeros((8, LANES), jnp.float32)
            for r in own_blocks():
                for j, v, av in stencil(state, c, r, DEEP, range(tiles)):
                    applied[c, j, pl.ds(r, DEEP), :] = av
                    acc += fold(v * av)
            quads.append(acc)
        return [whole(q) for q in quads]

    def halo_applied():
        for c in range(chains):
            for r, deep, lane_tiles in sides():
                for j, _, av in stencil(state, c, r, deep, lane_tiles):
                    applied[c, j, pl.ds(r, deep), :] = av

    others = sorted(range(1, devices), key=lambda d: -min(d, devices - d))

    def peer(d):
        other = lax.rem(me + d, devices)
        return (other // nc, lax.rem(other, nc))

    def send(k, quad, mass):
        out = scal[LOCAL][:1]
        for i, value in enumerate(quad + mass):
            out = jnp.where(seg == i, value[:1], out)
        payload[k] = out
        gathered[k, me] = out
        for d in others:
            pltpu.make_async_remote_copy(
                src_ref=payload.at[k], dst_ref=gathered.at[k, me],
                send_sem=sum_send.at[k], recv_sem=sum_recv.at[k],
                device_id=peer(d), device_id_type=MESH,
            ).start()

    def bulk(k):
        ref = gathered.at[k, pl.ds(0, devices - 1)]
        return pltpu.make_async_remote_copy(
            src_ref=ref, dst_ref=ref, send_sem=sum_send.at[k], recv_sem=sum_recv.at[k],
            device_id=peer(1), device_id_type=MESH,
        )

    def collect(k):
        bulk(k).wait_recv()
        summed = jnp.broadcast_to(jnp.sum(gathered[k], axis=0), (8, LANES))
        values = [
            jnp.broadcast_to(jnp.sum(jnp.where(lane == i * SEG, summed, 0.0), axis=1, keepdims=True), (8, LANES))
            for i in range(2 * chains + 1)
        ]
        return values[:chains], values[chains : 2 * chains], values[2 * chains]

    def kick_hyper(k, part):
        quad, mass, number = collect(k)
        for c in range(chains):
            aq = (0.5 / total) * (scal[TAU + c] * quad[c]) - 0.5
            ae = (scal[EXO + c] * mass[c] - number) * (1.0 / total)
            scal[VEQ + c] = scal[VEQ + c] - (part * h[c]) * aq
            scal[VEE + c] = scal[VEE + c] - (part * h[c]) * ae

    def drift_hyper():
        for c in range(chains):
            q = scal[HYQ + c] + h[c] * scal[VEQ + c]
            e = scal[HYE + c] + h[c] * scal[VEE + c]
            scal[HYQ + c] = q
            scal[HYE + c] = e
            scal[TAU + c] = jnp.exp(q)
            scal[EXO + c] = jnp.exp(e)

    def weights(part):
        xs = [(part * hh[c]) * scal[TAU + c] for c in range(chains)]
        ys = [(part * hh[c]) * scal[EXO + c] for c in range(chains)]
        return xs, ys

    def own_fresh(xs, ys):
        out = []
        for c in range(chains):
            x, y = xs[c][:1], ys[c][:1]
            acc = jnp.zeros((8, LANES), jnp.float32)
            for j in range(tiles):
                v = field_u[c, j, own, :] - x * applied[c, j, own, :] - y * intensity[c, j, own, :]
                value = jnp.exp(v)
                fresh[c, j] = v
                intensity[c, j, own, :] = value
                acc += fold(value)
            out.append(acc)
        return [whole(acc) for acc in out]

    def own_settle():
        for c in range(chains):
            for j in range(tiles):
                v = fresh[c, j]
                field_u[c, j, own, :] = (v + v) - state[c, j, own, :] + scaled[c, j, own, :]
                state[c, j, own, :] = v

    def halo_advance(xs, ys):
        for c in range(chains):
            x, y = xs[c][:1], ys[c][:1]
            for r, deep, lane_tiles in sides():
                rowset = pl.ds(r, deep)
                for j in lane_tiles:
                    v = field_u[c, j, rowset, :] - x * applied[c, j, rowset, :] - y * intensity[c, j, rowset, :]
                    field_u[c, j, rowset, :] = (v + v) - state[c, j, rowset, :] + scaled[c, j, rowset, :]
                    intensity[c, j, rowset, :] = jnp.exp(v)
                    state[c, j, rowset, :] = v

    def own_coefs(direct):
        for c in range(chains):
            sums = [jnp.zeros((8, LANES), jnp.float32)] * COEFS
            if not direct:
                for r in own_blocks():
                    rowset = pl.ds(r, DEEP)
                    for j, v, av in stencil(state, c, r, DEEP, range(tiles)):
                        au = (av + av) - applied[c, j, rowset, :] + scaled_applied[c, j, pl.ds(r - TOP, DEEP), :]
                        applied[c, j, rowset, :] = av
                        sums[0] += fold(field_u[c, j, rowset, :] * au)
                        sums[1] += fold(av * au)
                        sums[2] += fold(intensity[c, j, rowset, :] * au)
            yield c, sums

    def finish_coefs(direct, c, sums):
        for r in own_blocks():
            rowset = pl.ds(r, DEEP)
            if direct:
                for j, u, au in stencil(field_u, c, r, DEEP, range(tiles)):
                    sums[0] += fold(u * au)
                    sums[1] += fold(applied[c, j, rowset, :] * au)
                    sums[2] += fold(intensity[c, j, rowset, :] * au)
            for j, a, aa in stencil(applied, c, r, DEEP, range(tiles)):
                sums[3] += fold(a * aa)
                sums[4] += fold(intensity[c, j, rowset, :] * aa)
            for j, e, ae in stencil(intensity, c, r, DEEP, range(tiles)):
                sums[5] += fold(e * ae)
        for i in range(COEFS):
            scal[CO + COEFS * c + i] = whole(sums[i])

    def predicted(xs, ys):
        out = []
        for c in range(chains):
            k0, k1, k2, k3, k4, k5 = [scal[CO + COEFS * c + i] for i in range(COEFS)]
            x, y = xs[c], ys[c]
            out.append(k0 - 2.0 * (x * k1 + y * k2) + (x * (x * k3 + 2.0 * (y * k4)) + y * (y * k5)))
        return out

    for i in range(len(rounds)):
        pl.semaphore_wait(round_sem.at[i], len(rounds[i]))
        if i + 1 < len(rounds):
            tell(i + 1)
        if i == 0:
            for copy in remotes[:stage_one]:
                copy.wait_recv()
            for c in range(chains):
                for s in range(fold_one):
                    slot = s * chains + c
                    state[c, tiles, pl.ds(TOP + s * rows_one, rows_one), :] = unpack(
                        take_one[0], take_one[1], slot, slot
                    )
            quad = own_applied()
    send(0, quad, mass)

    xs, ys = weights(0.5)
    mass = own_fresh(xs, ys)

    for copy in remotes[stage_one:]:
        copy.wait_recv()
    for copy in remotes:
        copy.wait_send()

    strips = [(TOP + s * rows_two, rows_two, take_two.at[0], take_two.at[1], s, s) for s in range(fold_two)]
    strips += [
        (PAD, HALO, corner_two.at[0, 0], corner_two.at[1, 0], fold_two - 1, fold_two - 1),
        (TOP + rows, HALO, corner_two.at[0, 1], corner_two.at[1, 1], 0, 0),
    ]
    for r, deep, right, left, sr, sl in strips:
        for i in range(chains + 2):
            value = unpack(right[...], left[...], sr * (chains + 2) + i, sl * (chains + 2) + i)
            state[chains + i, tiles, pl.ds(r, deep), :] = value
    for vert, r, s in ((0, PAD, fold_one - 1), (1, TOP + rows, 0)):
        for c in range(chains):
            state[c, tiles, pl.ds(r, HALO), :] = unpack(
                corner_one[0, vert], corner_one[1, vert], s * chains + c, s * chains + c
            )
    for r, deep, lane_tiles in sides():
        rowset = pl.ds(r, deep)
        for j in lane_tiles:
            diagonal[j, rowset, :] = state[kap, j, rowset, :] + 4.0
            for c in range(chains):
                hc = hh[c] * state[cnt, j, rowset, :]
                scaled[c, j, rowset, :] = hc
                v = state[c, j, rowset, :]
                intensity[c, j, rowset, :] = jnp.exp(v)
                field_u[c, j, rowset, :] = v + (h[c] * state[chains + c, j, rowset, :] + 0.5 * hc)
    halo_applied()
    halo_advance(xs, ys)
    own_settle()
    send(1, own_applied(), mass)
    halo_applied()
    for r in own_blocks():
        for j, _, value in stencil(state, cnt, r, DEEP, range(tiles)):
            for c in range(chains):
                scaled_applied[c, j, pl.ds(r - TOP, DEEP), :] = hh[c] * value
    for c, sums in own_coefs(True):
        finish_coefs(True, c, sums)

    def step(k, carry):
        kick_hyper(k - 1, jnp.where(k == 1, 0.5, 1.0))
        drift_hyper()
        xs, ys = weights(1.0)
        mass = own_fresh(xs, ys)
        send(k + 1, predicted(xs, ys), mass)
        halo_advance(xs, ys)
        own_settle()
        pairs = list(own_coefs(False))
        halo_applied()
        for c, sums in pairs:
            finish_coefs(False, c, sums)
        return carry

    lax.fori_loop(1, STEPS, step, 0)

    for c in range(chains):
        for j in range(tiles):
            latent_out[c, :, pl.ds(j * LANES, LANES)] = state[c, j, own, :]
    kick_hyper(STEPS - 1, 1.0)
    drift_hyper()
    xs, ys = weights(0.5)
    for c in range(chains):
        x, y = xs[c][:1], ys[c][:1]
        for j in range(tiles):
            moved = field_u[c, j, own, :] - state[c, j, own, :] - 0.5 * scaled[c, j, own, :]
            moved = moved - x * applied[c, j, own, :] - y * intensity[c, j, own, :]
            momentum_out[c, :, pl.ds(j * LANES, LANES)] = moved * (1.0 / full(h[c])[:1])
    kick_hyper(STEPS, 0.5)

    out_row, out_col = sublane[:2, :2], lane[:2, :2]
    for high, low, ref in ((HYQ, HYE, hyper_out), (VEQ, VEE, velocity_out)):
        values = [[scal[base + c][:2, :2] for c in range(chains)] for base in (low, high)]
        pick = [jnp.where(out_col == 0, v[0], v[1]) for v in values]
        ref[...] = jnp.where(out_row == 0, pick[0], pick[1])

    def drain(k, carry):
        bulk(k).wait_send()
        return carry

    lax.fori_loop(0, STEPS + 1, drain, 0)


def hand_out(latent, momentum, hyper, velocity, latent_out, momentum_out, hyper_out, velocity_out, sems):
    copies = [
        pltpu.make_async_copy(latent, latent_out, sems.at[0]),
        pltpu.make_async_copy(momentum, momentum_out, sems.at[1]),
    ]
    for copy in copies:
        copy.start()
    hyper_out[...] = hyper[...]
    velocity_out[...] = velocity[...]
    for copy in copies:
        copy.wait()


def solution(mesh):
    nr, nc = mesh.shape["row"], mesh.shape["col"]
    devices = nr * nc

    def shards(latent, momentum, hyper_params, velocity, step_size, counts, kappa_field):
        chains, rows, cols = latent.shape
        tiles = cols // LANES
        deep = rows + 2 * TOP
        total = float(rows * nr * cols * nc)
        sizes = (nr, nc, chains, rows, tiles, total)
        anywhere = pl.BlockSpec(memory_space=pltpu.HBM)
        small = pl.BlockSpec(memory_space=pltpu.VMEM)
        arrays = 2 * chains + 2
        f32 = jnp.float32
        fold_one, fold_two = LANES // (SEG * chains), LANES // (SEG * (chains + 2))
        everywhere = pltpu.VMEM((chains, tiles + 1, deep, LANES), f32)
        inner = pltpu.VMEM((chains, tiles, rows, LANES), f32)
        strip_one = pltpu.VMEM((2, rows // fold_one, LANES), f32)
        strip_two = pltpu.VMEM((2, rows // fold_two, LANES), f32)
        corner = pltpu.VMEM((2, 2, HALO, LANES), f32)
        results = pl.pallas_call(
            functools.partial(kernel, sizes),
            out_shape=(
                jax.ShapeDtypeStruct(latent.shape, f32),
                jax.ShapeDtypeStruct(latent.shape, f32),
                jax.ShapeDtypeStruct(hyper_params.shape, f32),
                jax.ShapeDtypeStruct(velocity.shape, f32),
            ),
            in_specs=[anywhere] * 7,
            out_specs=(small,) * 4,
            scratch_shapes=[
                pltpu.VMEM((arrays, tiles + 1, deep, LANES), f32),
                everywhere,
                pltpu.VMEM((tiles + 1, deep, LANES), f32),
                everywhere,
                everywhere,
                everywhere,
                inner,
                inner,
                pltpu.VMEM((tiles, rows, LANES), jnp.int32),
                strip_one, strip_two, strip_one, strip_two, corner, corner,
                pltpu.VMEM((STEPS + 1, 1, LANES), f32),
                pltpu.VMEM((STEPS + 1, devices, 1, LANES), f32),
                pltpu.VMEM(((6 + COEFS) * chains + 1, 8, LANES), f32),
                pltpu.SMEM(hyper_params.shape, f32),
                pltpu.SMEM(velocity.shape, f32),
                pltpu.SMEM(step_size.shape, f32),
                pltpu.SemaphoreType.DMA((2 * tiles * (chains + 1) + 3,)),
                pltpu.SemaphoreType.DMA((18,)),
                pltpu.SemaphoreType.DMA((18,)),
                pltpu.SemaphoreType.DMA((STEPS + 1,)),
                pltpu.SemaphoreType.DMA((STEPS + 1,)),
                pltpu.SemaphoreType.REGULAR((len(signal_rounds(nr, nc)),)),
            ],
            compiler_params=pltpu.CompilerParams(
                collective_id=0, has_side_effects=True, vmem_limit_bytes=24 * 1024 * 1024
            ),
        )(*(pltpu.with_memory_space_constraint(x, pltpu.HBM) for x in (
            latent, momentum, counts, kappa_field, hyper_params, velocity, step_size
        )))
        return pl.pallas_call(
            hand_out,
            out_shape=[jax.ShapeDtypeStruct(x.shape, f32) for x in results],
            in_specs=[small] * 4,
            out_specs=[anywhere] * 2 + [small] * 2,
            scratch_shapes=[pltpu.SemaphoreType.DMA((2,))],
            compiler_params=pltpu.CompilerParams(vmem_limit_bytes=8 * 1024 * 1024),
        )(*results)

    placed = (
        P(None, "row", "col"),
        P(None, "row", "col"),
        P(),
        P(),
        P(),
        P("row", "col"),
        P("row", "col"),
    )
    return jax.shard_map(
        shards,
        mesh=mesh,
        in_specs=placed,
        out_specs=(P(None, "row", "col"), P(None, "row", "col"), P(), P()),
        check_vma=False,
    )
```

time: 53.2 us -> 46 us (0.86)
  Pallas kernels: 52.4 us -> 45.2 us
    pallas_call x1, Pallas kernels: 49.7 us -> 43.7 us  [shards(): pl.pallas_call(functools.partial(kernel, sizes), out_shape=(jax.ShapeDtyp...]
    pallas_call x1, Pallas kernels: 2.75 us -> 1.55 us  [shards(): pl.pallas_call(hand_out, out_shape=[jax.ShapeDtypeStruct(x.shape, f32) fo...]
where the time goes in v1:
time: 46 us; the launch traced here: 45.9 us
  Pallas kernels  45.2 us (98%)
  between operations  0.64 us (1%)
    pallas_call x1, Pallas kernels, shards(): pl.pallas_call(functools.partial(kernel, sizes), out_shape=(jax.ShapeDtyp...  43.7 us
    pallas_call x1, Pallas kernels, shards(): pl.pallas_call(hand_out, out_shape=[jax.ShapeDtypeStruct(x.shape, f32) fo...  1.55 us

profile of v1, /device:TPU:0, one launch (start us, length us, event | category | flops | bytes accessed | tf_op | source)
XLA Modules:
  0.0 45.9 jit_solution(9812459867641568926)
XLA Ops:
  0.6 43.7 %shard_map.102 = (f32[2,256,256]{2,1,0:T(8,128)S(1)}, f32[2,256,256]{2,1,0:T(8,128)S(1)}, f32[2,2]{1,0:T(2,128)S(1)}, f32[2,2]{1,0:T(2,128)S(1)}) custom-call(f32[2,256,256]{2,1,0:T(8,128)} %latent.1, f32[2,256,256]{2,1,0:T(8,128)} %momentum.1, s32[256,256]{1,0:T(8,128)} %counts.1, f32[256,256]{1,0:T(8,128)} %kappa.1, f32[2,2]{1,0:T(2,128)} %hyper_in.1, ...), custom_call_target="tpu_custom_call" | custom-call | tf_op jit(solution)/shard_map/pallas_call | solution.py:508
  44.3 1.6 %shard_map.103 = (f32[2,256,256]{2,1,0:T(8,128)}, f32[2,256,256]{2,1,0:T(8,128)}, f32[2,2]{1,0:T(2,128)}, f32[2,2]{1,0:T(2,128)}) custom-call(f32[2,256,256]{2,1,0:T(8,128)S(1)} %get-tuple-element.8.latent, f32[2,256,256]{2,1,0:T(8,128)S(1)} %get-tuple-element.9.momentum, f32[2,2]{1,0:T(2,128)S(1)} %get-tuple-element.10.hyper, ...), custom_call_target="tpu_custom_call" | custom-call | tf_op jit(solution)/shard_map/pallas_call | solution.py:548

commit v2 on v1

--- a/solution.py
+++ b/solution.py
@@ -10,6 +10,7 @@
 STEPS = 10
 HALO = 16
 EDGE = 8
+NEEDED = STEPS + 1
 PAD = 8
 TOP = PAD + HALO
 LANES = 128
@@ -32,7 +33,7 @@
     sizes, latent, momentum, counts, kappa, hyper_in, velocity_in, step_in,
     latent_out, momentum_out, hyper_out, velocity_out,
     state, field_u, diagonal, applied, intensity, scaled, scaled_applied, fresh, raw_counts,
-    pack_one, pack_two, take_one, take_two, corner_one, corner_two,
+    pack_one, pack_two, take_one, take_two, corner_out, corner_in,
     payload, gathered, scal, hyper, velocity, step_size,
     load_sem, halo_send, halo_recv, sum_send, sum_recv, round_sem,
 ):
@@ -121,7 +122,7 @@
         remotes.append(copy)
         copy.start()
 
-    vs, rest = pl.ds(0, chains), pl.ds(chains, chains + 2)
+    vs = pl.ds(0, chains)
     flat = pl.ds(0, tiles)
 
     def rowcopies(arrays, near_row, depth):
@@ -151,21 +152,32 @@
 
     for copy in loads[first_loads:]:
         copy.wait()
+    rowcopies(pl.ds(chains, chains + 1), 0, NEEDED - 1)
     counted = jnp.zeros((8, LANES), jnp.float32)
     for j in range(tiles):
         value = raw_counts[j].astype(jnp.float32)
         state[cnt, j, own, :] = value
         counted += fold(value)
+    for vert, start in ((1, TOP), (0, TOP + rows - HALO)):
+        heads = tails = None
+        for a in range(2 * chains + 2):
+            head = state[a, 0, pl.ds(start, HALO), :]
+            tail = pltpu.roll(state[a, tiles - 1, pl.ds(start, HALO), :], (a + 1) * SEG % LANES, 1)
+            if a:
+                head = pltpu.roll(head, a * SEG, 1)
+            heads = head if heads is None else jnp.where(seg == a, head, heads)
+            tails = tail if tails is None else jnp.where(seg == a, tail, tails)
+        corner_out[0, vert] = heads
+        corner_out[1, vert] = tails
+    rowcopies(pl.ds(cnt, 1), 0, NEEDED - 1)
+    for side, dc in ((0, -1), (1, 1)):
+        for vert, dr in ((1, -1), (0, 1)):
+            part = pl.ds(0 if vert else HALO - NEEDED, NEEDED)
+            remote(corner_out.at[side, vert, part], corner_in.at[side, vert, part], at(dr, dc))
+    rowcopies(vs, EDGE, NEEDED - EDGE)
     pack(pack_two, list(range(chains, 2 * chains + 2)), rows_two, fold_two)
-    rowcopies(vs, EDGE, HALO - EDGE)
     remote(pack_two.at[0], take_two.at[0], at(0, -1))
     remote(pack_two.at[1], take_two.at[1], at(0, 1))
-    rowcopies(rest, 0, HALO)
-    for side, dc in ((0, -1), (1, 1)):
-        for vert, dr in ((1, -1), (0, 1)):
-            for mine, theirs, deep in ((pack_one, corner_one, rows_one), (pack_two, corner_two, rows_two)):
-                start = 0 if vert else deep - HALO
-                remote(mine.at[side, pl.ds(start, HALO)], theirs.at[side, vert], at(dr, dc))
 
     h = [step_size[c] for c in range(chains)]
     hh = [h[c] * h[c] for c in range(chains)]
@@ -393,20 +405,15 @@
     for copy in remotes:
         copy.wait_send()
 
-    strips = [(TOP + s * rows_two, rows_two, take_two.at[0], take_two.at[1], s, s) for s in range(fold_two)]
-    strips += [
-        (PAD, HALO, corner_two.at[0, 0], corner_two.at[1, 0], fold_two - 1, fold_two - 1),
-        (TOP + rows, HALO, corner_two.at[0, 1], corner_two.at[1, 1], 0, 0),
-    ]
-    for r, deep, right, left, sr, sl in strips:
+    for s in range(fold_two):
         for i in range(chains + 2):
-            value = unpack(right[...], left[...], sr * (chains + 2) + i, sl * (chains + 2) + i)
-            state[chains + i, tiles, pl.ds(r, deep), :] = value
-    for vert, r, s in ((0, PAD, fold_one - 1), (1, TOP + rows, 0)):
-        for c in range(chains):
-            state[c, tiles, pl.ds(r, HALO), :] = unpack(
-                corner_one[0, vert], corner_one[1, vert], s * chains + c, s * chains + c
+            slot = s * (chains + 2) + i
+            state[chains + i, tiles, pl.ds(TOP + s * rows_two, rows_two), :] = unpack(
+                take_two[0], take_two[1], slot, slot
             )
+    for vert, r in ((0, PAD), (1, TOP + rows)):
+        for a in range(2 * chains + 2):
+            state[a, tiles, pl.ds(r, HALO), :] = unpack(corner_in[0, vert], corner_in[1, vert], a, a)
     for r, deep, lane_tiles in sides():
         rowset = pl.ds(r, deep)
         for j in lane_tiles:
@@ -472,15 +479,12 @@
     lax.fori_loop(0, STEPS + 1, drain, 0)
 
 
-def hand_out(latent, momentum, hyper, velocity, latent_out, momentum_out, hyper_out, velocity_out, sems):
-    copies = [
-        pltpu.make_async_copy(latent, latent_out, sems.at[0]),
-        pltpu.make_async_copy(momentum, momentum_out, sems.at[1]),
-    ]
+def hand_out(*refs):
+    count = (len(refs) - 1) // 2
+    sems = refs[-1]
+    copies = [pltpu.make_async_copy(refs[i], refs[count + i], sems.at[i]) for i in range(count)]
     for copy in copies:
         copy.start()
-    hyper_out[...] = hyper[...]
-    velocity_out[...] = velocity[...]
     for copy in copies:
         copy.wait()
 
@@ -533,8 +537,8 @@
                 pltpu.SMEM(velocity.shape, f32),
                 pltpu.SMEM(step_size.shape, f32),
                 pltpu.SemaphoreType.DMA((2 * tiles * (chains + 1) + 3,)),
-                pltpu.SemaphoreType.DMA((18,)),
-                pltpu.SemaphoreType.DMA((18,)),
+                pltpu.SemaphoreType.DMA((16,)),
+                pltpu.SemaphoreType.DMA((16,)),
                 pltpu.SemaphoreType.DMA((STEPS + 1,)),
                 pltpu.SemaphoreType.DMA((STEPS + 1,)),
                 pltpu.SemaphoreType.REGULAR((len(signal_rounds(nr, nc)),)),
@@ -549,8 +553,8 @@
             hand_out,
             out_shape=[jax.ShapeDtypeStruct(x.shape, f32) for x in results],
             in_specs=[small] * 4,
-            out_specs=[anywhere] * 2 + [small] * 2,
-            scratch_shapes=[pltpu.SemaphoreType.DMA((2,))],
+            out_specs=[pl.BlockSpec(memory_space=pl.ANY)] * 4,
+            scratch_shapes=[pltpu.SemaphoreType.DMA((4,))],
             compiler_params=pltpu.CompilerParams(vmem_limit_bytes=8 * 1024 * 1024),
         )(*results)
 

time: 46 us -> 42.9 us (0.933)
  Pallas kernels: 45.2 us -> 42.1 us
    pallas_call x1, Pallas kernels: 43.7 us -> 41.1 us  [shards(): pl.pallas_call(functools.partial(kernel, sizes), out_shape=(jax.ShapeDtyp...]
    pallas_call x1, Pallas kernels: 1.55 us -> 1.01 us  [shards(): pl.pallas_call(hand_out, out_shape=[jax.ShapeDtypeStruct(x.shape, f32) fo...]
where the time goes in v2:
time: 42.9 us; the launch traced here: 42.8 us
  Pallas kernels  42.1 us (98%)
  between operations  0.64 us (1%)
    pallas_call x1, Pallas kernels, shards(): pl.pallas_call(functools.partial(kernel, sizes), out_shape=(jax.ShapeDtyp...  41.1 us
    pallas_call x1, Pallas kernels, shards(): pl.pallas_call(hand_out, out_shape=[jax.ShapeDtypeStruct(x.shape, f32) fo...  1.01 us

profile of v2, /device:TPU:0, one launch (start us, length us, event | category | flops | bytes accessed | tf_op | source)
XLA Modules:
  0.0 42.8 jit_solution(8338308768804647144)
XLA Ops:
  0.6 41.1 %shard_map.102 = (f32[2,256,256]{2,1,0:T(8,128)S(1)}, f32[2,256,256]{2,1,0:T(8,128)S(1)}, f32[2,2]{1,0:T(2,128)S(1)}, f32[2,2]{1,0:T(2,128)S(1)}) custom-call(f32[2,256,256]{2,1,0:T(8,128)} %latent.1, f32[2,256,256]{2,1,0:T(8,128)} %momentum.1, s32[256,256]{1,0:T(8,128)} %counts.1, f32[256,256]{1,0:T(8,128)} %kappa.1, f32[2,2]{1,0:T(2,128)} %hyper_in.1, ...), custom_call_target="tpu_custom_call" | custom-call | tf_op jit(solution)/shard_map/pallas_call | solution.py:512
  41.8 1.0 %shard_map.103 = (f32[2,256,256]{2,1,0:T(8,128)}, f32[2,256,256]{2,1,0:T(8,128)}, f32[2,2]{1,0:T(2,128)}, f32[2,2]{1,0:T(2,128)}) custom-call(f32[2,256,256]{2,1,0:T(8,128)S(1)} %get-tuple-element.8.refs_0_, f32[2,256,256]{2,1,0:T(8,128)S(1)} %get-tuple-element.9.refs_1_, f32[2,2]{1,0:T(2,128)S(1)} %get-tuple-element.10.refs_2_, ...), custom_call_target="tpu_custom_call" | custom-call | tf_op jit(solution)/shard_map/pallas_call | solution.py:552

commit v3 on v2

--- a/solution.py
+++ b/solution.py
@@ -15,16 +15,14 @@
 TOP = PAD + HALO
 LANES = 128
 SEG = 16
-MESH = pl.DeviceIdType.MESH
+MESH, LOGICAL = pl.DeviceIdType.MESH, pl.DeviceIdType.LOGICAL
 COEFS = 6
 
 
-def signal_rounds(nr, nc):
+def signal_rounds(nr):
     rounds, reach = [], 1
-    while reach < nr // 2 or reach < nc // 2:
-        rs = (0, reach, -reach) if reach < nr // 2 else (0,)
-        cs = (0, reach, -reach) if reach < nc // 2 else (0,)
-        rounds.append([(r, c) for r in rs for c in cs if (r, c) != (0, 0)])
+    while reach < nr // 2:
+        rounds.append(reach)
         reach *= 2
     return rounds
 
@@ -33,7 +31,7 @@
     sizes, latent, momentum, counts, kappa, hyper_in, velocity_in, step_in,
     latent_out, momentum_out, hyper_out, velocity_out,
     state, field_u, diagonal, applied, intensity, scaled, scaled_applied, fresh, raw_counts,
-    pack_one, pack_two, take_one, take_two, corner_out, corner_in,
+    padded, half, pack_one, pack_two, take_one, take_two, corner_out, corner_in,
     payload, gathered, scal, hyper, velocity, step_size,
     load_sem, halo_send, halo_recv, sum_send, sum_recv, round_sem,
 ):
@@ -65,13 +63,19 @@
     for copy in loads:
         copy.start()
 
+    def wrap(d):
+        other = me + d % devices
+        return jnp.where(other < devices, other, other - devices)
+
     def at(dr, dc):
         return (lax.rem(row + (dr + nr), nr), lax.rem(col + (dc + nc), nc))
 
-    near = [(r, c) for r in (0, 1, -1) for c in (0, 1, -1) if (r, c) != (0, 0)]
     barrier = pltpu.get_barrier_semaphore()
-    for r, c in near:
-        pl.semaphore_signal(barrier, inc=1, device_id=at(r, c), device_id_type=MESH)
+    near = [lax.rem(row + r, nr) * nc + c for r in (1, nr - 1) for c in range(nc)]
+    near += [row * nc + jnp.where(col + c < nc, col + c, col + c - nc) for c in range(1, nc)]
+    for other in near:
+        pl.semaphore_signal(barrier, inc=1, device_id=other, device_id_type=LOGICAL)
+    others = [wrap(d) for d in sorted(range(1, devices), key=lambda d: -min(d, devices - d))]
 
     lane = lax.broadcasted_iota(jnp.int32, (8, LANES), 1)
     sublane = lax.broadcasted_iota(jnp.int32, (8, LANES), 0)
@@ -142,11 +146,11 @@
     rowcopies(vs, 0, EDGE)
     stage_one = len(remotes)
 
-    rounds = signal_rounds(nr, nc)
+    rounds = signal_rounds(nr)
 
     def tell(i):
-        for r, c in rounds[i]:
-            pl.semaphore_signal(round_sem.at[i], inc=1, device_id=at(r, c), device_id_type=MESH)
+        for r in (rounds[i], -rounds[i]):
+            pl.semaphore_signal(round_sem.at[i], inc=1, device_id=at(r, 0), device_id_type=MESH)
 
     tell(0)
 
@@ -206,7 +210,9 @@
             acc = fold(value) if acc is None else acc + fold(value)
         mass.append(whole(acc))
     for j in range(tiles):
-        diagonal[j, own, :] = state[kap, j, own, :] + 4.0
+        diag = state[kap, j, own, :] + 4.0
+        diagonal[j, own, :] = diag
+        half[j] = 0.5 * diag
         for c in range(chains):
             hc = hh[c] * state[cnt, j, own, :]
             scaled[c, j, own, :] = hc
@@ -228,6 +234,16 @@
             out.append((j, at_tile[j], diagonal[j, rowset, :] * at_tile[j] - beside))
         return out
 
+    def half_stencil(ref, c, r, deep):
+        rowset = pl.ds(r, deep)
+        at_tile = [ref[c, j, rowset, :] for j in everything]
+        to_left = [pltpu.roll(x, LANES - 1, 1) for x in at_tile]
+        out = []
+        for j in range(tiles):
+            beside = jnp.where(last, to_left[j + 1], to_left[j]) + ref[c, j, pl.ds(r + 1, deep), :]
+            out.append((j, at_tile[j], half[j, pl.ds(r - TOP, deep), :] * at_tile[j] - beside))
+        return out
+
     DEEP = 64
 
     def own_blocks():
@@ -237,28 +253,22 @@
         out = [(TOP + i * DEEP, DEEP, [tiles]) for i in range(rows // DEEP)]
         return out + [(PAD, HALO, everything), (TOP + rows, HALO, everything)]
 
-    def own_applied():
+    def own_applied(ref):
         quads = []
         for c in range(chains):
             acc = jnp.zeros((8, LANES), jnp.float32)
             for r in own_blocks():
-                for j, v, av in stencil(state, c, r, DEEP, range(tiles)):
+                for j, v, av in stencil(ref, c, r, DEEP, range(tiles)):
                     applied[c, j, pl.ds(r, DEEP), :] = av
                     acc += fold(v * av)
             quads.append(acc)
-        return [whole(q) for q in quads]
+        return quads
 
     def halo_applied():
         for c in range(chains):
             for r, deep, lane_tiles in sides():
                 for j, _, av in stencil(state, c, r, deep, lane_tiles):
                     applied[c, j, pl.ds(r, deep), :] = av
-
-    others = sorted(range(1, devices), key=lambda d: -min(d, devices - d))
-
-    def peer(d):
-        other = lax.rem(me + d, devices)
-        return (other // nc, lax.rem(other, nc))
 
     def send(k, quad, mass):
         out = scal[LOCAL][:1]
@@ -266,18 +276,18 @@
             out = jnp.where(seg == i, value[:1], out)
         payload[k] = out
         gathered[k, me] = out
-        for d in others:
+        for other in others:
             pltpu.make_async_remote_copy(
                 src_ref=payload.at[k], dst_ref=gathered.at[k, me],
                 send_sem=sum_send.at[k], recv_sem=sum_recv.at[k],
-                device_id=peer(d), device_id_type=MESH,
+                device_id=other, device_id_type=LOGICAL,
             ).start()
 
     def bulk(k):
         ref = gathered.at[k, pl.ds(0, devices - 1)]
         return pltpu.make_async_remote_copy(
             src_ref=ref, dst_ref=ref, send_sem=sum_send.at[k], recv_sem=sum_recv.at[k],
-            device_id=peer(1), device_id_type=MESH,
+            device_id=others[0], device_id_type=LOGICAL,
         )
 
     def collect(k):
@@ -365,13 +375,13 @@
                     sums[0] += fold(u * au)
                     sums[1] += fold(applied[c, j, rowset, :] * au)
                     sums[2] += fold(intensity[c, j, rowset, :] * au)
-            for j, a, aa in stencil(applied, c, r, DEEP, range(tiles)):
-                sums[3] += fold(a * aa)
-                sums[4] += fold(intensity[c, j, rowset, :] * aa)
-            for j, e, ae in stencil(intensity, c, r, DEEP, range(tiles)):
-                sums[5] += fold(e * ae)
+            for (j, a, ta), (_, e, te) in zip(half_stencil(applied, c, r, DEEP), half_stencil(intensity, c, r, DEEP)):
+                sums[3] += fold(a * ta)
+                sums[4] += fold(e * ta + a * te)
+                sums[5] += fold(e * te)
         for i in range(COEFS):
-            scal[CO + COEFS * c + i] = whole(sums[i])
+            total_i = whole(sums[i])
+            scal[CO + COEFS * c + i] = total_i + total_i if i in (3, 5) else total_i
 
     def predicted(xs, ys):
         out = []
@@ -381,21 +391,48 @@
             out.append(k0 - 2.0 * (x * k1 + y * k2) + (x * (x * k3 + 2.0 * (y * k4)) + y * (y * k5)))
         return out
 
+    for c in range(chains):
+        for r in (TOP - 8, TOP + rows):
+            for j in range(tiles):
+                padded[c, j, pl.ds(r, 8), :] = jnp.zeros((8, LANES), jnp.float32)
+        padded[c, tiles, own, :] = jnp.zeros((rows, LANES), jnp.float32)
+        for j in range(tiles):
+            padded[c, j, own, :] = state[c, j, own, :]
+    quad = own_applied(padded)
+    place = lane_row % SEG
+
     for i in range(len(rounds)):
-        pl.semaphore_wait(round_sem.at[i], len(rounds[i]))
+        pl.semaphore_wait(round_sem.at[i], 2)
         if i + 1 < len(rounds):
             tell(i + 1)
-        if i == 0:
-            for copy in remotes[:stage_one]:
-                copy.wait_recv()
-            for c in range(chains):
-                for s in range(fold_one):
-                    slot = s * chains + c
-                    state[c, tiles, pl.ds(TOP + s * rows_one, rows_one), :] = unpack(
-                        take_one[0], take_one[1], slot, slot
-                    )
-            quad = own_applied()
+    for copy in remotes[:stage_one]:
+        copy.wait_recv()
+    across = jnp.where(place == SEG - 1, pack_one[1] * pltpu.roll(take_one[0], SEG - 1, 1), 0.0)
+    across += jnp.where(place == 0, pack_one[0] * pltpu.roll(take_one[1], LANES - SEG + 1, 1), 0.0)
+    across = fold(across)
+    for c in range(chains):
+        along = sum(
+            state[c, j, pl.ds(TOP, 1), :] * state[c, j, pl.ds(TOP - 1, 1), :]
+            + state[c, j, pl.ds(TOP + rows - 1, 1), :] * state[c, j, pl.ds(TOP + rows, 1), :]
+            for j in range(tiles)
+        )
+        quad[c] = whole(quad[c] - jnp.where(seg % chains == c, across, 0.0) - jnp.where(sublane == 0, along, 0.0))
     send(0, quad, mass)
+
+    for c in range(chains):
+        for s in range(fold_one):
+            slot = s * chains + c
+            part = pl.ds(TOP + s * rows_one, rows_one)
+            side = unpack(take_one[0], take_one[1], slot, slot)
+            state[c, tiles, part, :] = side
+            applied[c, 0, part, :] = applied[c, 0, part, :] - jnp.where(first, pltpu.roll(side, 1, 1), 0.0)
+            applied[c, tiles - 1, part, :] = applied[c, tiles - 1, part, :] - jnp.where(
+                last, pltpu.roll(side, LANES - 1, 1), 0.0
+            )
+        for j in range(tiles):
+            for here, there in ((TOP, TOP - 1), (TOP + rows - 1, TOP + rows)):
+                here, there = pl.ds(here, 1), pl.ds(there, 1)
+                applied[c, j, here, :] = applied[c, j, here, :] - state[c, j, there, :]
 
     xs, ys = weights(0.5)
     mass = own_fresh(xs, ys)
@@ -427,7 +464,7 @@
     halo_applied()
     halo_advance(xs, ys)
     own_settle()
-    send(1, own_applied(), mass)
+    send(1, [whole(q) for q in own_applied(state)], mass)
     halo_applied()
     for r in own_blocks():
         for j, _, value in stencil(state, cnt, r, DEEP, range(tiles)):
@@ -529,6 +566,8 @@
                 inner,
                 inner,
                 pltpu.VMEM((tiles, rows, LANES), jnp.int32),
+                everywhere,
+                pltpu.VMEM((tiles, rows, LANES), f32),
                 strip_one, strip_two, strip_one, strip_two, corner, corner,
                 pltpu.VMEM((STEPS + 1, 1, LANES), f32),
                 pltpu.VMEM((STEPS + 1, devices, 1, LANES), f32),
@@ -541,7 +580,7 @@
                 pltpu.SemaphoreType.DMA((16,)),
                 pltpu.SemaphoreType.DMA((STEPS + 1,)),
                 pltpu.SemaphoreType.DMA((STEPS + 1,)),
-                pltpu.SemaphoreType.REGULAR((len(signal_rounds(nr, nc)),)),
+                pltpu.SemaphoreType.REGULAR((len(signal_rounds(nr)),)),
             ],
             compiler_params=pltpu.CompilerParams(
                 collective_id=0, has_side_effects=True, vmem_limit_bytes=24 * 1024 * 1024

time: 42.9 us -> 42.6 us (level)
  no operation moved by 1% of the time
where the time goes in v3:
time: 42.6 us; the launch traced here: 42.5 us
  Pallas kernels  41.8 us (98%)
  between operations  0.64 us (2%)
    pallas_call x1, Pallas kernels, shards(): pl.pallas_call(functools.partial(kernel, sizes), out_shape=(jax.ShapeDtyp...  40.8 us
    pallas_call x1, Pallas kernels, shards(): pl.pallas_call(hand_out, out_shape=[jax.ShapeDtypeStruct(x.shape, f32) fo...  1.01 us

profile of v3, /device:TPU:0, one launch (start us, length us, event | category | flops | bytes accessed | tf_op | source)
XLA Modules:
  0.0 42.5 jit_solution(11765488740922677668)
XLA Ops:
  0.6 40.8 %shard_map.102 = (f32[2,256,256]{2,1,0:T(8,128)S(1)}, f32[2,256,256]{2,1,0:T(8,128)S(1)}, f32[2,2]{1,0:T(2,128)S(1)}, f32[2,2]{1,0:T(2,128)S(1)}) custom-call(f32[2,256,256]{2,1,0:T(8,128)} %latent.1, f32[2,256,256]{2,1,0:T(8,128)} %momentum.1, s32[256,256]{1,0:T(8,128)} %counts.1, f32[256,256]{1,0:T(8,128)} %kappa.1, f32[2,2]{1,0:T(2,128)} %hyper_in.1, ...), custom_call_target="tpu_custom_call" | custom-call | tf_op jit(solution)/shard_map/pallas_call | solution.py:549
  41.5 1.0 %shard_map.103 = (f32[2,256,256]{2,1,0:T(8,128)}, f32[2,256,256]{2,1,0:T(8,128)}, f32[2,2]{1,0:T(2,128)}, f32[2,2]{1,0:T(2,128)}) custom-call(f32[2,256,256]{2,1,0:T(8,128)S(1)} %get-tuple-element.8.refs_0_, f32[2,256,256]{2,1,0:T(8,128)S(1)} %get-tuple-element.9.refs_1_, f32[2,2]{1,0:T(2,128)S(1)} %get-tuple-element.10.refs_2_, ...), custom_call_target="tpu_custom_call" | custom-call | tf_op jit(solution)/shard_map/pallas_call | solution.py:591

commit v4 on v3

--- a/solution.py
+++ b/solution.py
@@ -156,7 +156,6 @@
 
     for copy in loads[first_loads:]:
         copy.wait()
-    rowcopies(pl.ds(chains, chains + 1), 0, NEEDED - 1)
     counted = jnp.zeros((8, LANES), jnp.float32)
     for j in range(tiles):
         value = raw_counts[j].astype(jnp.float32)
@@ -173,15 +172,20 @@
             tails = tail if tails is None else jnp.where(seg == a, tail, tails)
         corner_out[0, vert] = heads
         corner_out[1, vert] = tails
-    rowcopies(pl.ds(cnt, 1), 0, NEEDED - 1)
+    rest = pl.ds(chains, chains + 2)
+    rowcopies(rest, 0, 1)
     for side, dc in ((0, -1), (1, 1)):
         for vert, dr in ((1, -1), (0, 1)):
             part = pl.ds(0 if vert else HALO - NEEDED, NEEDED)
             remote(corner_out.at[side, vert, part], corner_in.at[side, vert, part], at(dr, dc))
+    early = remotes[stage_one:]
+    rowcopies(rest, 1, NEEDED - 2)
     rowcopies(vs, EDGE, NEEDED - EDGE)
+    bulk_rows = remotes[stage_one + len(early) :]
     pack(pack_two, list(range(chains, 2 * chains + 2)), rows_two, fold_two)
     remote(pack_two.at[0], take_two.at[0], at(0, -1))
     remote(pack_two.at[1], take_two.at[1], at(0, 1))
+    early += remotes[-2:]
 
     h = [step_size[c] for c in range(chains)]
     hh = [h[c] * h[c] for c in range(chains)]
@@ -249,9 +253,14 @@
     def own_blocks():
         return [TOP + i * DEEP for i in range(rows // DEEP)]
 
+    def flanks():
+        return [(r, DEEP, [tiles]) for r in own_blocks()]
+
+    def ends():
+        return [(PAD, HALO, everything), (TOP + rows, HALO, everything)]
+
     def sides():
-        out = [(TOP + i * DEEP, DEEP, [tiles]) for i in range(rows // DEEP)]
-        return out + [(PAD, HALO, everything), (TOP + rows, HALO, everything)]
+        return flanks() + ends()
 
     def own_applied(ref):
         quads = []
@@ -264,9 +273,9 @@
             quads.append(acc)
         return quads
 
-    def halo_applied():
-        for c in range(chains):
-            for r, deep, lane_tiles in sides():
+    def halo_applied(regions):
+        for c in range(chains):
+            for r, deep, lane_tiles in regions:
                 for j, _, av in stencil(state, c, r, deep, lane_tiles):
                     applied[c, j, pl.ds(r, deep), :] = av
 
@@ -437,11 +446,8 @@
     xs, ys = weights(0.5)
     mass = own_fresh(xs, ys)
 
-    for copy in remotes[stage_one:]:
+    for copy in early:
         copy.wait_recv()
-    for copy in remotes:
-        copy.wait_send()
-
     for s in range(fold_two):
         for i in range(chains + 2):
             slot = s * (chains + 2) + i
@@ -451,21 +457,49 @@
     for vert, r in ((0, PAD), (1, TOP + rows)):
         for a in range(2 * chains + 2):
             state[a, tiles, pl.ds(r, HALO), :] = unpack(corner_in[0, vert], corner_in[1, vert], a, a)
-    for r, deep, lane_tiles in sides():
-        rowset = pl.ds(r, deep)
-        for j in lane_tiles:
-            diagonal[j, rowset, :] = state[kap, j, rowset, :] + 4.0
-            for c in range(chains):
-                hc = hh[c] * state[cnt, j, rowset, :]
-                scaled[c, j, rowset, :] = hc
-                v = state[c, j, rowset, :]
-                intensity[c, j, rowset, :] = jnp.exp(v)
-                field_u[c, j, rowset, :] = v + (h[c] * state[chains + c, j, rowset, :] + 0.5 * hc)
-    halo_applied()
+    def halo_start(regions):
+        for r, deep, lane_tiles in regions:
+            rowset = pl.ds(r, deep)
+            for j in lane_tiles:
+                diagonal[j, rowset, :] = state[kap, j, rowset, :] + 4.0
+                for c in range(chains):
+                    hc = hh[c] * state[cnt, j, rowset, :]
+                    scaled[c, j, rowset, :] = hc
+                    v = state[c, j, rowset, :]
+                    intensity[c, j, rowset, :] = jnp.exp(v)
+                    field_u[c, j, rowset, :] = v + (h[c] * state[chains + c, j, rowset, :] + 0.5 * hc)
+
+    halo_start(flanks())
+    halo_applied(flanks())
+    for c in range(chains):
+        x, y = xs[c][:1], ys[c][:1]
+        padded[c, tiles, own, :] = (
+            field_u[c, tiles, own, :] - x * applied[c, tiles, own, :] - y * intensity[c, tiles, own, :]
+        )
+        for r in (TOP - 1, TOP + rows):
+            line = pl.ds(r, 1)
+            cells = [state[c, j, line, :] for j in everything]
+            to_right, to_left = [pltpu.roll(z, 1, 1) for z in cells], [pltpu.roll(z, LANES - 1, 1) for z in cells]
+            for j in range(tiles):
+                beside = jnp.where(first, to_right[(j - 1) % (tiles + 1)], to_right[j])
+                beside += jnp.where(last, to_left[j + 1], to_left[j])
+                beside += state[c, j, pl.ds(r - 1, 1), :] + state[c, j, pl.ds(r + 1, 1), :]
+                av = (state[kap, j, line, :] + 4.0) * cells[j] - beside
+                u = cells[j] + (h[c] * state[chains + c, j, line, :] + 0.5 * (hh[c] * state[cnt, j, line, :]))
+                padded[c, j, line, :] = u - x * av - y * jnp.exp(cells[j])
+        for j in range(tiles):
+            padded[c, j, own, :] = fresh[c, j]
+    send(1, [whole(q) for q in own_applied(padded)], mass)
+
+    for copy in bulk_rows:
+        copy.wait_recv()
+    for copy in remotes:
+        copy.wait_send()
+    halo_start(ends())
+    halo_applied(ends())
     halo_advance(xs, ys)
     own_settle()
-    send(1, [whole(q) for q in own_applied(state)], mass)
-    halo_applied()
+    halo_applied(sides())
     for r in own_blocks():
         for j, _, value in stencil(state, cnt, r, DEEP, range(tiles)):
             for c in range(chains):
@@ -482,7 +516,7 @@
         halo_advance(xs, ys)
         own_settle()
         pairs = list(own_coefs(False))
-        halo_applied()
+        halo_applied(sides())
         for c, sums in pairs:
             finish_coefs(False, c, sums)
         return carry

time: 42.6 us -> 41.5 us (0.974)
  Pallas kernels: 41.8 us -> 40.7 us
    pallas_call x1, Pallas kernels: 40.8 us -> 39.7 us  [shards(): pl.pallas_call(functools.partial(kernel, sizes), out_shape=(jax.ShapeDtyp...]
where the time goes in v4:
time: 41.5 us; the launch traced here: 41.4 us
  Pallas kernels  40.7 us (98%)
  between operations  0.64 us (2%)
    pallas_call x1, Pallas kernels, shards(): pl.pallas_call(functools.partial(kernel, sizes), out_shape=(jax.ShapeDtyp...  39.7 us
    pallas_call x1, Pallas kernels, shards(): pl.pallas_call(hand_out, out_shape=[jax.ShapeDtypeStruct(x.shape, f32) fo...  1.01 us

profile of v4, /device:TPU:0, one launch (start us, length us, event | category | flops | bytes accessed | tf_op | source)
XLA Modules:
  0.0 41.4 jit_solution(10606184987389852668)
XLA Ops:
  0.6 39.7 %shard_map.102 = (f32[2,256,256]{2,1,0:T(8,128)S(1)}, f32[2,256,256]{2,1,0:T(8,128)S(1)}, f32[2,2]{1,0:T(2,128)S(1)}, f32[2,2]{1,0:T(2,128)S(1)}) custom-call(f32[2,256,256]{2,1,0:T(8,128)} %latent.1, f32[2,256,256]{2,1,0:T(8,128)} %momentum.1, s32[256,256]{1,0:T(8,128)} %counts.1, f32[256,256]{1,0:T(8,128)} %kappa.1, f32[2,2]{1,0:T(2,128)} %hyper_in.1, ...), custom_call_target="tpu_custom_call" | custom-call | tf_op jit(solution)/shard_map/pallas_call | solution.py:583
  40.3 1.0 %shard_map.103 = (f32[2,256,256]{2,1,0:T(8,128)}, f32[2,256,256]{2,1,0:T(8,128)}, f32[2,2]{1,0:T(2,128)}, f32[2,2]{1,0:T(2,128)}) custom-call(f32[2,256,256]{2,1,0:T(8,128)S(1)} %get-tuple-element.8.refs_0_, f32[2,256,256]{2,1,0:T(8,128)S(1)} %get-tuple-element.9.refs_1_, f32[2,2]{1,0:T(2,128)S(1)} %get-tuple-element.10.refs_2_, ...), custom_call_target="tpu_custom_call" | custom-call | tf_op jit(solution)/shard_map/pallas_call | solution.py:625

commit v5 on v4

--- a/solution.py
+++ b/solution.py
@@ -67,6 +67,10 @@
         other = me + d % devices
         return jnp.where(other < devices, other, other - devices)
 
+    def flip(x, mask):
+        bits = [b for b in (1 << i for i in range(mask.bit_length())) if mask & b]
+        return x + sum(b - 2 * b * (x // b % 2) for b in bits)
+
     def at(dr, dc):
         return (lax.rem(row + (dr + nr), nr), lax.rem(col + (dc + nc), nc))
 
@@ -75,7 +79,12 @@
     near += [row * nc + jnp.where(col + c < nc, col + c, col + c - nc) for c in range(1, nc)]
     for other in near:
         pl.semaphore_signal(barrier, inc=1, device_id=other, device_id_type=LOGICAL)
-    others = [wrap(d) for d in sorted(range(1, devices), key=lambda d: -min(d, devices - d))]
+    if nr & (nr - 1) or nc & (nc - 1):
+        others = [wrap(d) for d in range(1, devices)]
+    else:
+        pairs = [(r, c) for r in range(nr) for c in range(nc) if r or c]
+        pairs.sort(key=lambda p: (p[1] & 1) - 2 * (p[0] + bin(p[1] >> 1).count("1")))
+        others = [flip(row, r) * nc + flip(col, c) for r, c in pairs]
 
     lane = lax.broadcasted_iota(jnp.int32, (8, LANES), 1)
     sublane = lax.broadcasted_iota(jnp.int32, (8, LANES), 0)
@@ -535,10 +544,9 @@
             moved = field_u[c, j, own, :] - state[c, j, own, :] - 0.5 * scaled[c, j, own, :]
             moved = moved - x * applied[c, j, own, :] - y * intensity[c, j, own, :]
             momentum_out[c, :, pl.ds(j * LANES, LANES)] = moved * (1.0 / full(h[c])[:1])
-    kick_hyper(STEPS, 0.5)
-
     out_row, out_col = sublane[:2, :2], lane[:2, :2]
-    for high, low, ref in ((HYQ, HYE, hyper_out), (VEQ, VEE, velocity_out)):
+
+    def show(high, low, ref):
         values = [[scal[base + c][:2, :2] for c in range(chains)] for base in (low, high)]
         pick = [jnp.where(out_col == 0, v[0], v[1]) for v in values]
         ref[...] = jnp.where(out_row == 0, pick[0], pick[1])
@@ -547,7 +555,11 @@
         bulk(k).wait_send()
         return carry
 
-    lax.fori_loop(0, STEPS + 1, drain, 0)
+    show(HYQ, HYE, hyper_out)
+    lax.fori_loop(0, STEPS, drain, 0)
+    kick_hyper(STEPS, 0.5)
+    show(VEQ, VEE, velocity_out)
+    drain(STEPS, 0)
 
 
 def hand_out(*refs):

time: 41.5 us -> 40.7 us (0.981)
  Pallas kernels: 40.7 us -> 39.9 us
    pallas_call x1, Pallas kernels: 39.7 us -> 38.9 us  [shards(): pl.pallas_call(functools.partial(kernel, sizes), out_shape=(jax.ShapeDtyp...]
where the time goes in v5:
time: 40.7 us; the launch traced here: 40.6 us
  Pallas kernels  39.9 us (98%)
  between operations  0.64 us (2%)
    pallas_call x1, Pallas kernels, shards(): pl.pallas_call(functools.partial(kernel, sizes), out_shape=(jax.ShapeDtyp...  38.9 us
    pallas_call x1, Pallas kernels, shards(): pl.pallas_call(hand_out, out_shape=[jax.ShapeDtypeStruct(x.shape, f32) fo...  1.01 us

profile of v5, /device:TPU:0, one launch (start us, length us, event | category | flops | bytes accessed | tf_op | source)
XLA Modules:
  0.0 40.6 jit_solution(7629257218670523896)
XLA Ops:
  0.6 38.9 %shard_map.102 = (f32[2,256,256]{2,1,0:T(8,128)S(1)}, f32[2,256,256]{2,1,0:T(8,128)S(1)}, f32[2,2]{1,0:T(2,128)S(1)}, f32[2,2]{1,0:T(2,128)S(1)}) custom-call(f32[2,256,256]{2,1,0:T(8,128)} %latent.1, f32[2,256,256]{2,1,0:T(8,128)} %momentum.1, s32[256,256]{1,0:T(8,128)} %counts.1, f32[256,256]{1,0:T(8,128)} %kappa.1, f32[2,2]{1,0:T(2,128)} %hyper_in.1, ...), custom_call_target="tpu_custom_call" | custom-call | tf_op jit(solution)/shard_map/pallas_call | solution.py:595
  39.6 1.0 %shard_map.103 = (f32[2,256,256]{2,1,0:T(8,128)}, f32[2,256,256]{2,1,0:T(8,128)}, f32[2,2]{1,0:T(2,128)}, f32[2,2]{1,0:T(2,128)}) custom-call(f32[2,256,256]{2,1,0:T(8,128)S(1)} %get-tuple-element.8.refs_0_, f32[2,256,256]{2,1,0:T(8,128)S(1)} %get-tuple-element.9.refs_1_, f32[2,2]{1,0:T(2,128)S(1)} %get-tuple-element.10.refs_2_, ...), custom_call_target="tpu_custom_call" | custom-call | tf_op jit(solution)/shard_map/pallas_call | solution.py:637

commit v6 on v5

--- a/solution.py
+++ b/solution.py
@@ -45,23 +45,23 @@
     own = pl.ds(TOP, rows)
     everything = range(tiles + 1)
 
-    smalls = [(hyper_in, hyper), (velocity_in, velocity), (step_in, step_size)]
-    vloads, loads = [], []
-    for c in range(chains):
-        for j in range(tiles):
-            cols = pl.ds(j * LANES, LANES)
-            vloads.append((latent.at[c, :, cols], state.at[c, j, own, :]))
-            loads.append((momentum.at[c, :, cols], state.at[chains + c, j, own, :]))
+    vs, flat = pl.ds(0, chains), pl.ds(0, tiles)
+    groups = [[], [], []]
     for j in range(tiles):
         cols = pl.ds(j * LANES, LANES)
-        loads.append((kappa.at[:, cols], state.at[kap, j, own, :]))
-        loads.append((counts.at[:, cols], raw_counts.at[j]))
-    first_loads = len(vloads)
-    loads = [
-        pltpu.make_async_copy(s, d, load_sem.at[i]) for i, (s, d) in enumerate(vloads + loads + smalls)
-    ]
-    for copy in loads:
-        copy.start()
+        for c in range(chains):
+            groups[0].append((latent.at[c, :, cols], state.at[c, j, own, :]))
+            groups[1].append((momentum.at[c, :, cols], state.at[chains + c, j, own, :]))
+        groups[1].append((kappa.at[:, cols], state.at[kap, j, own, :]))
+        groups[2].append((counts.at[:, cols], raw_counts.at[j]))
+    groups += [[(hyper_in, hyper)], [(velocity_in, velocity)], [(step_in, step_size)]]
+    for i, group in enumerate(groups):
+        for source, target in group:
+            pltpu.make_async_copy(source, target, load_sem.at[i]).start()
+    targets = [state.at[vs, flat, own, :], state.at[pl.ds(chains, chains + 1), flat, own, :], raw_counts]
+    targets += [hyper, velocity, step_size]
+    loads = [pltpu.make_async_copy(target, target, load_sem.at[i]) for i, target in enumerate(targets)]
+    first_loads = 1
 
     def wrap(d):
         other = me + d % devices
@@ -135,8 +135,6 @@
         remotes.append(copy)
         copy.start()
 
-    vs = pl.ds(0, chains)
-    flat = pl.ds(0, tiles)
 
     def rowcopies(arrays, near_row, depth):
         remote(
@@ -293,24 +291,24 @@
         for i, value in enumerate(quad + mass):
             out = jnp.where(seg == i, value[:1], out)
         payload[k] = out
-        gathered[k, me] = out
+        gathered[k, pl.ds(me, 1), :] = out
         for other in others:
             pltpu.make_async_remote_copy(
-                src_ref=payload.at[k], dst_ref=gathered.at[k, me],
-                send_sem=sum_send.at[k], recv_sem=sum_recv.at[k],
+                src_ref=payload.at[k], dst_ref=gathered.at[k, pl.ds(me, 1), :],
+                send_sem=sum_send, recv_sem=sum_recv.at[k],
                 device_id=other, device_id_type=LOGICAL,
             ).start()
 
     def bulk(k):
-        ref = gathered.at[k, pl.ds(0, devices - 1)]
+        ref = gathered.at[k, pl.ds(0, devices - 1), :]
         return pltpu.make_async_remote_copy(
-            src_ref=ref, dst_ref=ref, send_sem=sum_send.at[k], recv_sem=sum_recv.at[k],
+            src_ref=ref, dst_ref=ref, send_sem=sum_send, recv_sem=sum_recv.at[0 if isinstance(k, pl.Slice) else k],
             device_id=others[0], device_id_type=LOGICAL,
         )
 
     def collect(k):
         bulk(k).wait_recv()
-        summed = jnp.broadcast_to(jnp.sum(gathered[k], axis=0), (8, LANES))
+        summed = jnp.broadcast_to(jnp.sum(gathered[k], axis=0, keepdims=True), (8, LANES))
         values = [
             jnp.broadcast_to(jnp.sum(jnp.where(lane == i * SEG, summed, 0.0), axis=1, keepdims=True), (8, LANES))
             for i in range(2 * chains + 1)
@@ -551,15 +549,10 @@
         pick = [jnp.where(out_col == 0, v[0], v[1]) for v in values]
         ref[...] = jnp.where(out_row == 0, pick[0], pick[1])
 
-    def drain(k, carry):
-        bulk(k).wait_send()
-        return carry
-
     show(HYQ, HYE, hyper_out)
-    lax.fori_loop(0, STEPS, drain, 0)
     kick_hyper(STEPS, 0.5)
     show(VEQ, VEE, velocity_out)
-    drain(STEPS, 0)
+    bulk(pl.ds(0, STEPS + 1)).wait_send()
 
 
 def hand_out(*refs):
@@ -616,15 +609,15 @@
                 pltpu.VMEM((tiles, rows, LANES), f32),
                 strip_one, strip_two, strip_one, strip_two, corner, corner,
                 pltpu.VMEM((STEPS + 1, 1, LANES), f32),
-                pltpu.VMEM((STEPS + 1, devices, 1, LANES), f32),
+                pltpu.VMEM((STEPS + 1, devices, LANES), f32),
                 pltpu.VMEM(((6 + COEFS) * chains + 1, 8, LANES), f32),
                 pltpu.SMEM(hyper_params.shape, f32),
                 pltpu.SMEM(velocity.shape, f32),
                 pltpu.SMEM(step_size.shape, f32),
-                pltpu.SemaphoreType.DMA((2 * tiles * (chains + 1) + 3,)),
+                pltpu.SemaphoreType.DMA((6,)),
                 pltpu.SemaphoreType.DMA((16,)),
                 pltpu.SemaphoreType.DMA((16,)),
-                pltpu.SemaphoreType.DMA((STEPS + 1,)),
+                pltpu.SemaphoreType.DMA,
                 pltpu.SemaphoreType.DMA((STEPS + 1,)),
                 pltpu.SemaphoreType.REGULAR((len(signal_rounds(nr)),)),
             ],

time: 40.7 us -> 40.4 us (level)
  no operation moved by 1% of the time
where the time goes in v6:
time: 40.4 us; the launch traced here: 40.3 us
  Pallas kernels  39.6 us (98%)
  between operations  0.64 us (2%)
    pallas_call x1, Pallas kernels, shards(): pl.pallas_call(functools.partial(kernel, sizes), out_shape=(jax.ShapeDtyp...  38.6 us
    pallas_call x1, Pallas kernels, shards(): pl.pallas_call(hand_out, out_shape=[jax.ShapeDtypeStruct(x.shape, f32) fo...  1.01 us

profile of v6, /device:TPU:0, one launch (start us, length us, event | category | flops | bytes accessed | tf_op | source)
XLA Modules:
  0.0 40.3 jit_solution(12404503700217142049)
XLA Ops:
  0.6 38.6 %shard_map.102 = (f32[2,256,256]{2,1,0:T(8,128)S(1)}, f32[2,256,256]{2,1,0:T(8,128)S(1)}, f32[2,2]{1,0:T(2,128)S(1)}, f32[2,2]{1,0:T(2,128)S(1)}) custom-call(f32[2,256,256]{2,1,0:T(8,128)} %latent.1, f32[2,256,256]{2,1,0:T(8,128)} %momentum.1, s32[256,256]{1,0:T(8,128)} %counts.1, f32[256,256]{1,0:T(8,128)} %kappa.1, f32[2,2]{1,0:T(2,128)} %hyper_in.1, ...), custom_call_target="tpu_custom_call" | custom-call | tf_op jit(solution)/shard_map/pallas_call | solution.py:588
  39.2 1.0 %shard_map.103 = (f32[2,256,256]{2,1,0:T(8,128)}, f32[2,256,256]{2,1,0:T(8,128)}, f32[2,2]{1,0:T(2,128)}, f32[2,2]{1,0:T(2,128)}) custom-call(f32[2,256,256]{2,1,0:T(8,128)S(1)} %get-tuple-element.8.refs_0_, f32[2,256,256]{2,1,0:T(8,128)S(1)} %get-tuple-element.9.refs_1_, f32[2,2]{1,0:T(2,128)S(1)} %get-tuple-element.10.refs_2_, ...), custom_call_target="tpu_custom_call" | custom-call | tf_op jit(solution)/shard_map/pallas_call | solution.py:630

commit v7 on v6

--- a/solution.py
+++ b/solution.py
@@ -93,7 +93,9 @@
     first, last = lane_row == 0, lane_row == LANES - 1
 
     def fold(x):
-        return sum(x[8 * i : 8 * i + 8] for i in range(x.shape[0] // 8))
+        parts = [x[8 * i : 8 * i + 8] for i in range(x.shape[0] // 8)]
+        lines = [sum(parts[i::4]) for i in range(4)] if len(parts) > 8 else parts
+        return sum(lines)
 
     def whole(x):
         return jnp.broadcast_to(jnp.sum(jnp.sum(x, axis=0, keepdims=True), axis=1, keepdims=True), (8, LANES))

time: 40.4 us -> 40.3 us (level)
  no operation moved by 1% of the time
where the time goes in v7:
time: 40.3 us; the launch traced here: 40.2 us
  Pallas kernels  39.5 us (98%)
  between operations  0.64 us (2%)
    pallas_call x1, Pallas kernels, shards(): pl.pallas_call(functools.partial(kernel, sizes), out_shape=(jax.ShapeDtyp...  38.5 us
    pallas_call x1, Pallas kernels, shards(): pl.pallas_call(hand_out, out_shape=[jax.ShapeDtypeStruct(x.shape, f32) fo...  1.01 us

profile of v7, /device:TPU:0, one launch (start us, length us, event | category | flops | bytes accessed | tf_op | source)
XLA Modules:
  0.0 40.2 jit_solution(8522512671082665611)
XLA Ops:
  0.6 38.5 %shard_map.102 = (f32[2,256,256]{2,1,0:T(8,128)S(1)}, f32[2,256,256]{2,1,0:T(8,128)S(1)}, f32[2,2]{1,0:T(2,128)S(1)}, f32[2,2]{1,0:T(2,128)S(1)}) custom-call(f32[2,256,256]{2,1,0:T(8,128)} %latent.1, f32[2,256,256]{2,1,0:T(8,128)} %momentum.1, s32[256,256]{1,0:T(8,128)} %counts.1, f32[256,256]{1,0:T(8,128)} %kappa.1, f32[2,2]{1,0:T(2,128)} %hyper_in.1, ...), custom_call_target="tpu_custom_call" | custom-call | tf_op jit(solution)/shard_map/pallas_call | solution.py:590
  39.1 1.0 %shard_map.103 = (f32[2,256,256]{2,1,0:T(8,128)}, f32[2,256,256]{2,1,0:T(8,128)}, f32[2,2]{1,0:T(2,128)}, f32[2,2]{1,0:T(2,128)}) custom-call(f32[2,256,256]{2,1,0:T(8,128)S(1)} %get-tuple-element.8.refs_0_, f32[2,256,256]{2,1,0:T(8,128)S(1)} %get-tuple-element.9.refs_1_, f32[2,2]{1,0:T(2,128)S(1)} %get-tuple-element.10.refs_2_, ...), custom_call_target="tpu_custom_call" | custom-call | tf_op jit(solution)/shard_map/pallas_call | solution.py:632
